TPU v7x, 32 devices: a whole 2x2x4 slice. The times are simulated.
32 devices in a mesh: section: 2 (over y), dp: 16 (over z, x, core).
Axes of the slice: x: 2, y: 2, z: 4, core: 2. Of those that a mesh axis runs over, the one named last changes fastest.
Arguments:
- residuals: float32 [8, 128, 4096], P('section', 'dp'), may hold values from -100 to 100, as said below
- owners: int32 [32], replicated, may hold values from 0 to 31, each once
Outputs:
- harvest: bfloat16 [128, 8, 4096], P(('section', 'dp'))
Inputs may be any that keep to these rules, and one draw needn't show every extreme that they name: `owners`: a permutation of the block numbers. `residuals`: real-valued activations.
All inputs are finite; a program needn't handle non-finite values.
Results may differ from a plain program's by a relative error of at most 0.0004.
Values may be sent and summed in bfloat16 or wider, within the bound.
A program may use at most 64 MiB of HBM per device.

v0:
```python
import jax
import jax.numpy as jnp
from jax import lax
from jax.sharding import PartitionSpec as P


def on_device(residuals, owners):
    layer_dev, tok_dev, features = residuals.shape
    groups = lax.axis_size("dp")
    sections = lax.axis_size("section")
    centered = residuals - jnp.mean(residuals, axis=2, keepdims=True)
    partial_value = jnp.sum(centered * centered, axis=(1, 2))
    energy = lax.psum(partial_value, "dp")
    layer_scale = 1.0 / jnp.sqrt(energy / (tok_dev * groups * features) + 1.0)
    normed = (centered * layer_scale[:, None, None]).astype(jnp.bfloat16).transpose(1, 0, 2)
    spread_rows = lax.all_to_all(normed, "dp", split_axis=2, concat_axis=0, tiled=True)
    token_total = spread_rows.shape[0]
    narrow = spread_rows.shape[2]
    blocks_all = owners.shape[0]
    block_len = token_total // blocks_all
    inverse = (
        jnp.zeros((blocks_all,), jnp.int32).at[owners].set(jnp.arange(blocks_all, dtype=jnp.int32))
    )
    ordered = spread_rows.reshape(blocks_all, block_len, layer_dev, narrow)[inverse]
    ordered = ordered.reshape(sections, groups, block_len, layer_dev, narrow)
    received = lax.all_to_all(
        lax.all_to_all(ordered, "section", split_axis=0, concat_axis=3, tiled=True),
        "dp",
        split_axis=1,
        concat_axis=4,
        tiled=True,
    )
    return received.reshape(block_len, layer_dev * sections, narrow * groups)


def solution(mesh):
    in_specs = (P("section", "dp", None), P())
    out_specs = P(("section", "dp"), None, None)
    return jax.shard_map(
        on_device, mesh=mesh, in_specs=in_specs, out_specs=out_specs, check_vma=False
    )
```

profile of v0, /device:TPU:0, one launch (start us, length us, event | category | flops | bytes accessed | tf_op | source)
XLA Modules:
  0.0 97.8 jit_solution(439982995596775943)
XLA Ops:
  0.0 1.2 %reduce_sum.18 = f32[4,8]{1,0:T(4,128)S(1)} reduce(f32[4,8,4096]{2,1,0:T(8,128)} %param.2, f32[]{:T(128)} %constant.2.clone.1), dimensions={2}, to_apply=%region_0.0 | reduce | flops 131040 | bytes 524420 | tf_op jit(solution)/shard_map/reduce_sum | solution.py:11
  1.2 1.3 %multiply_reduce_fusion = f32[4]{0:T(128)S(1)} fusion(f32[4,8,4096]{2,1,0:T(8,128)} %param.2, f32[4,8]{1,0:T(4,128)S(1)} %broadcast_multiply_fusion), kind=kLoop, calls=%fused_computation.3 | loop fusion | flops 393212 | bytes 524432 | tf_op jit(solution)/shard_map/reduce_sum | solution.py:12
  2.4 34.9 %psum.7 = f32[4]{0:T(128)S(1)} all-reduce(f32[4]{0:T(128)S(1)} %multiply_reduce_fusion), channel_id=1, replica_groups=mesh['section'=2,'dp'=16] {'dp'}, use_global_device_ids=true, to_apply=%region_2.0 | all-reduce | flops 4 | bytes 32 | tf_op jit(solution)/shard_map/psum | solution.py:13
  37.4 1.2 %fusion = bf16[8,4,4096]{2,0,1:T(8,128)(2,1)S(1)} fusion(f32[4,8,4096]{2,1,0:T(8,128)} %param.2, f32[4]{0:T(128)S(1)} %add_rsqrt_fusion, f32[4,8]{1,0:T(4,128)S(1)} %broadcast_multiply_fusion), kind=kLoop, calls=%fused_computation.4 | loop fusion | flops 393216 | bytes 786576 | tf_op jit(solution)/shard_map/transpose | solution.py:15
  38.5 0.0 copy-start
  38.5 4.6 %copy.25 = bf16[8,4,4096]{0,1,2:T(4,128)(2,1)} copy(bf16[8,4,4096]{2,0,1:T(8,128)(2,1)S(1)} %fusion) | data formatting | bytes 524288 | tf_op jit(solution)/shard_map/transpose | solution.py:15
  43.1 6.4 %reshape.39 = bf16[16,2,4096]{2,1,0:T(2,128)(2,1)} reshape(bf16[4096,4,8]{2,1,0:T(4,128)(2,1)} %bitcast.19) | data formatting | bytes 524288
  49.6 3.5 %all-to-all-start = ((bf16[16,2,4096]{2,1,0:T(2,128)(2,1)}), bf16[16,2,4096]{2,1,0:T(2,128)(2,1)S(1)}, u32[]{:S(2)}, u32[]{:S(2)}) async-start(bf16[16,2,4096]{2,1,0:T(2,128)(2,1)} %reshape.39), calls=%async_computation | async-start | bytes 524288 | tf_op jit(solution)/shard_map/all_to_all | solution.py:16
  53.1 0.0 copy-done
  53.1 0.7 scatter_custom_fusion
  53.8 9.2 %all-to-all-done = bf16[16,2,4096]{2,1,0:T(2,128)(2,1)S(1)} async-done(((bf16[16,2,4096]{2,1,0:T(2,128)(2,1)}), bf16[16,2,4096]{2,1,0:T(2,128)(2,1)S(1)}, u32[]{:S(2)}, u32[]{:S(2)}) %all-to-all-start) | async-done | bytes 262176 | tf_op jit(solution)/shard_map/all_to_all | solution.py:16
  63.1 5.9 %reshape.40 = bf16[4096,4,8]{2,1,0:T(4,128)(2,1)} reshape(bf16[16,2,4096]{2,1,0:T(2,128)(2,1)S(1)} %all-to-all-done) | data formatting | bytes 524288
  69.0 6.0 %copy.26 = bf16[8,4,16,256]{3,1,0,2:T(4,128)(2,1)S(1)} copy(bf16[8,4,16,256]{0,1,3,2:T(4,128)(2,1)} %bitcast.20) | data formatting | bytes 524288 | tf_op jit(solution)/shard_map/all_to_all | solution.py:16
  75.0 0.8 gather_fusion
  75.8 0.1 copy.28
  75.8 7.9 %all_to_all.48 = bf16[2,16,4,4,256]{4,1,3,2,0:T(8,128)(2,1)S(1)} all-to-all(bf16[2,16,4,4,256]{4,1,3,2,0:T(8,128)(2,1)S(1)} %copy.28), channel_id=1, replica_groups=mesh['section'=2,'dp'=16] {'section'}, dimensions={0} | all-to-all | bytes 524288 | tf_op jit(solution)/shard_map/all_to_all | solution.py:27
  83.8 0.1 copy.30
  83.8 13.0 %all_to_all.49 = bf16[1,16,4,8,256]{4,3,2,0,1:T(8,128)(2,1)S(1)} all-to-all(bf16[1,16,4,8,256]{4,3,2,0,1:T(8,128)(2,1)S(1)} %copy.30), channel_id=1, replica_groups=mesh['section'=2,'dp'=16] {'dp'}, dimensions={1} | all-to-all | bytes 524288 | tf_op jit(solution)/shard_map/all_to_all | solution.py:26
  96.9 0.1 copy.31
  97.0 0.8 reshape.18
  (7 shorter events, 0.0 us)
Async XLA Ops:
  38.5 14.6 %copy-start = (s32[32]{0:T(128)S(1)}, s32[32]{0:T(128)}, u32[]{:S(2)}) copy-start(s32[32]{0:T(128)} %param.3) | copy-start | bytes 388
  49.6 13.5 %all-to-all-start = ((bf16[16,2,4096]{2,1,0:T(2,128)(2,1)}), bf16[16,2,4096]{2,1,0:T(2,128)(2,1)S(1)}, u32[]{:S(2)}, u32[]{:S(2)}) async-start(bf16[16,2,4096]{2,1,0:T(2,128)(2,1)} %reshape.39), calls=%async_computation | async-start | bytes 524288 | tf_op jit(solution)/shard_map/all_to_all | solution.py:16
where the time goes:
time: 98.5 us; the launch traced here: 97.8 us
  blocking collectives  55.8 us (57%)
  local copies, waits for them, and re-layouts  25.5 us (26%)
  waiting for transfers between devices  9.24 us (9%)
  other arithmetic  3.63 us (4%)
  starting transfers between devices  3.53 us (4%)
    psum x1, blocking collectives, on_device(): energy = lax.psum(partial_value, 'dp')  34.9 us
    all_to_all x1, blocking collectives, on_device(): lax.all_to_all(lax.all_to_all(ordered, 'section', split_axis=0, concat_ax...  13 us
    unnamed x4, local copies, waits for them, and re-layouts  12.4 us
    all_to_all x1, waiting for transfers between devices, on_device(): lax.all_to_all(normed, 'dp', split_axis=2, concat_axis=0, tiled=True)  9.24 us
    all_to_all x1, blocking collectives, on_device(): lax.all_to_all(ordered, 'section', split_axis=0, concat_axis=3, tiled=True)  7.89 us
    all_to_all x1, local copies, waits for them, and re-layouts, on_device(): lax.all_to_all(normed, 'dp', split_axis=2, concat_axis=0, tiled=True)  5.97 us
    transpose x1, local copies, waits for them, and re-layouts, on_device(): (centered * layer_scale[:, None, None]).astype(jnp.bfloat16)  4.59 us
    all_to_all x1, starting transfers between devices, on_device(): lax.all_to_all(normed, 'dp', split_axis=2, concat_axis=0, tiled=True)  3.53 us
  transfers between devices with their start and end apart: 1, of which 1 were waited for; matrix products, arithmetic and copies ran while one was open for 1% of the time, Pallas kernels for 0%

commit v1 on v0

v1 whole, which is shorter than its diff:
```python
import functools

import jax
import jax.numpy as jnp
from jax import lax
from jax.experimental import pallas as pl
from jax.experimental.pallas import tpu as pltpu
from jax.sharding import PartitionSpec as P

MESH = pl.DeviceIdType.MESH
LANES = 128
SUBLANES = 8


def harvest_kernel(sections, groups, x_hbm, owners, out_ref, inverse, xv, centered, part, parts, s1, s2, r2,
                   x_sem, e_send, e_recv, send1, recv1, send2, recv2, *r1):
    layers, tokens, features = x_hbm.shape
    chunks, blocks, rows, _ = s1.shape
    width = features // groups
    block_len = rows // layers
    per_dev = tokens // block_len
    devices = sections * groups
    section, group = lax.axis_index("section"), lax.axis_index("dp")
    me = section * groups + group

    load = pltpu.make_async_copy(x_hbm, xv, x_sem)
    load.start()
    barrier = pltpu.get_barrier_semaphore()

    def peer_of(k):
        return lax.rem(group + k, groups)

    for k in range(1, groups):
        pl.semaphore_signal(barrier, inc=1, device_id=(section, peer_of(k)), device_id_type=MESH)
    for k in range(1, sections):
        pl.semaphore_signal(barrier, inc=1, device_id=(lax.rem(section + k, sections), group), device_id_type=MESH)

    load.wait()
    per_tile = SUBLANES // layers
    acc = jnp.zeros((SUBLANES, LANES), jnp.float32)
    for g in range(tokens // per_tile):
        x8 = jnp.concatenate([xv[:, g * per_tile + i, :] for i in range(per_tile)], axis=0)
        c = x8 - jnp.sum(x8, axis=1, keepdims=True) * (1.0 / features)
        centered[g * SUBLANES:(g + 1) * SUBLANES, :] = c
        sq = c * c
        for f in range(features // LANES):
            acc = acc + sq[:, f * LANES:(f + 1) * LANES]
    part[...] = acc
    parts[group] = acc

    pl.semaphore_wait(barrier, groups + sections - 2)
    for k in range(1, groups):
        pltpu.make_async_remote_copy(
            src_ref=part, dst_ref=parts.at[group], send_sem=e_send, recv_sem=e_recv,
            device_id=(section, peer_of(k)), device_id_type=MESH).start()

    @pl.loop(0, blocks)
    def _(o):
        found = jnp.int32(0)
        for b in range(blocks):
            found = jnp.where(owners[b] == o, jnp.int32(b), found)
        inverse[o] = found

    others = pl.ds(0, groups - 1)
    energy_wait = pltpu.make_async_remote_copy(
        src_ref=parts.at[others], dst_ref=parts.at[others], send_sem=e_send, recv_sem=e_recv,
        device_id=(section, peer_of(1)), device_id_type=MESH)
    energy_wait.wait_recv()
    total = parts[0]
    for g in range(1, groups):
        total = total + parts[g]
    row = jnp.sum(total, axis=1, keepdims=True)
    energy = row
    for i in range(1, per_tile):
        energy = energy + jnp.concatenate([row[i * layers:], row[:i * layers]], axis=0)
    scale = 1.0 / jnp.sqrt(energy * (1.0 / (tokens * groups * features)) + 1.0)
    scale = jnp.concatenate([scale] * (rows // SUBLANES), axis=0)

    for k in range(chunks):
        for d in range(groups):
            for j in range(per_dev):
                lane = d * width + k * LANES
                s1[k, d * per_dev + j] = (
                    centered[j * rows:(j + 1) * rows, lane:lane + LANES] * scale).astype(jnp.bfloat16)
        mine = pl.ds(group * per_dev, per_dev)
        for p in range(1, groups):
            d = peer_of(p)
            pltpu.make_async_remote_copy(
                src_ref=s1.at[k, pl.ds(d * per_dev, per_dev)], dst_ref=r1[k].at[mine],
                send_sem=send1.at[k], recv_sem=recv1.at[k],
                device_id=(section, d), device_id_type=MESH).start()
        r1[k][mine] = s1[k, mine]

    for k in range(chunks):
        span = pl.ds(0, (groups - 1) * per_dev)
        pltpu.make_async_remote_copy(
            src_ref=r1[k].at[span], dst_ref=r1[k].at[span], send_sem=send1.at[k], recv_sem=recv1.at[k],
            device_id=(section, peer_of(1)), device_id_type=MESH).wait_recv()
        for o in range(devices):
            s2[k, o] = r1[k][inverse[o]]
        for p in range(1, devices):
            o = lax.rem(me + p, devices)
            pltpu.make_async_remote_copy(
                src_ref=s2.at[k, o], dst_ref=r2.at[k, me],
                send_sem=send2.at[k], recv_sem=recv2.at[k],
                device_id=(o // groups, lax.rem(o, groups)), device_id_type=MESH).start()
        r2[k, me] = s2[k, me]

    for k in range(chunks):
        span = pl.ds(0, devices - 1)
        pltpu.make_async_remote_copy(
            src_ref=r2.at[k, span], dst_ref=r2.at[k, span], send_sem=send2.at[k], recv_sem=recv2.at[k],
            device_id=(section, peer_of(1)), device_id_type=MESH).wait_recv()
        for d in range(groups):
            got = [r2[k, s * groups + d].astype(jnp.float32) for s in range(sections)]
            lane = d * width + k * LANES
            for i in range(block_len):
                out_ref[i, :, lane:lane + LANES] = jnp.concatenate(
                    [v[i * layers:(i + 1) * layers] for v in got], axis=0).astype(jnp.bfloat16)

    energy_wait.wait_send()
    for k in range(chunks):
        span = pl.ds(0, (groups - 1) * per_dev)
        pltpu.make_async_remote_copy(
            src_ref=s1.at[k, span], dst_ref=r1[k].at[span], send_sem=send1.at[k], recv_sem=recv1.at[k],
            device_id=(section, peer_of(1)), device_id_type=MESH).wait_send()
        span = pl.ds(0, devices - 1)
        pltpu.make_async_remote_copy(
            src_ref=s2.at[k, span], dst_ref=r2.at[k, span], send_sem=send2.at[k], recv_sem=recv2.at[k],
            device_id=(section, peer_of(1)), device_id_type=MESH).wait_send()


def solution(mesh):
    sections, groups = mesh.shape["section"], mesh.shape["dp"]

    def on_device(residuals, owners):
        layers, tokens, features = residuals.shape
        blocks = owners.shape[0]
        block_len = tokens * groups // blocks
        rows = block_len * layers
        chunks = features // groups // LANES
        tiles = (chunks, blocks, rows, LANES)
        dma = pltpu.SemaphoreType.DMA
        return pl.pallas_call(
            functools.partial(harvest_kernel, sections, groups),
            out_shape=jax.ShapeDtypeStruct((block_len, layers * sections, features), jnp.bfloat16),
            in_specs=[pl.BlockSpec(memory_space=pl.ANY), pl.BlockSpec(memory_space=pltpu.SMEM)],
            out_specs=pl.BlockSpec(memory_space=pltpu.VMEM),
            scratch_shapes=[
                pltpu.SMEM((blocks,), jnp.int32),
                pltpu.VMEM((layers, tokens, features), jnp.float32),
                pltpu.VMEM((layers * tokens, features), jnp.float32),
                pltpu.VMEM((SUBLANES, LANES), jnp.float32),
                pltpu.VMEM((groups, SUBLANES, LANES), jnp.float32),
                pltpu.VMEM(tiles, jnp.bfloat16),
                pltpu.VMEM(tiles, jnp.bfloat16),
                pltpu.VMEM(tiles, jnp.bfloat16),
                dma, dma, dma,
                dma((chunks,)), dma((chunks,)), dma((chunks,)), dma((chunks,)),
                *[pltpu.VMEM(tiles[1:], jnp.bfloat16) for _ in range(chunks)],
            ],
            compiler_params=pltpu.CompilerParams(collective_id=0, has_side_effects=True),
            name="harvest",
        )(residuals, owners)

    in_specs = (P("section", "dp", None), P())
    out_specs = P(("section", "dp"), None, None)
    return jax.shard_map(on_device, mesh=mesh, in_specs=in_specs, out_specs=out_specs, check_vma=False)
```

time: 98.5 us -> 27.1 us (0.28)
  blocking collectives: 55.8 us -> 0 us
  Pallas kernels: 0 us -> 25.3 us
  local copies, waits for them, and re-layouts: 25.5 us -> 1.67 us
  waiting for transfers between devices: 9.24 us -> 0 us
  other arithmetic: 3.63 us -> 0 us
  starting transfers between devices: 3.53 us -> 0 us
    psum x1 -> x0, blocking collectives: 34.9 us -> none  [on_device(): energy = lax.psum(partial_value, 'dp')]
    pallas_call x0 -> x1, Pallas kernels: none -> 25.3 us  [on_device(): pl.pallas_call(functools.partial(harvest_kernel, sections, groups), out_s...]
    all_to_all x2 -> x0, blocking collectives: 20.9 us -> none  [the longest x1 13 us: on_device(): lax.all_to_all(lax.all_to_all(ordered, 'section', split_axis=0, concat_ax...]
    unnamed x4 -> x1, local copies, waits for them, and re-layouts: 12.4 us -> 1.67 us
    all_to_all x1 -> x0, waiting for transfers between devices: 9.24 us -> none  [on_device(): lax.all_to_all(normed, 'dp', split_axis=2, concat_axis=0, tiled=True)]
    all_to_all x4 -> x0, local copies, waits for them, and re-layouts: 6.22 us -> none  [the longest x1 5.97 us: on_device(): lax.all_to_all(normed, 'dp', split_axis=2, concat_axis=0, tiled=True)]
    transpose x1 -> x0, local copies, waits for them, and re-layouts: 4.59 us -> none  [on_device(): (centered * layer_scale[:, None, None]).astype(jnp.bfloat16)]
    all_to_all x1 -> x0, starting transfers between devices: 3.53 us -> none  [on_device(): lax.all_to_all(normed, 'dp', split_axis=2, concat_axis=0, tiled=True)]
  transfers between devices with their start and end apart: 1 -> 0, of which waited for: 1 -> 0; matrix products, arithmetic and copies ran while one was open for 1% -> 0% of each run, Pallas kernels for 0% -> 0%
where the time goes in v1:
time: 27.1 us; the launch traced here: 26.9 us
  Pallas kernels  25.3 us (93%)
  local copies, waits for them, and re-layouts  1.67 us (6%)
    pallas_call x1, Pallas kernels, on_device(): pl.pallas_call(functools.partial(harvest_kernel, sections, groups), out_s...  25.3 us
    unnamed x1, local copies, waits for them, and re-layouts  1.67 us

profile of v1, /device:TPU:0, one launch (start us, length us, event | category | flops | bytes accessed | tf_op | source)
XLA Modules:
  0.0 26.9 jit_solution(1659006340405378184)
XLA Ops:
  0.0 25.3 %harvest.1 = bf16[4,8,4096]{2,1,0:T(8,128)(2,1)} custom-call(f32[4,8,4096]{2,1,0:T(8,128)} %x_hbm.1, s32[32]{0:T(128)} %owners.1), custom_call_target="tpu_custom_call" | custom-call | tf_op jit(solution)/shard_map/harvest/pallas_call | solution.py:144
  25.3 1.7 %copy.4 = bf16[4,8,4096]{2,1,0:T(8,128)(2,1)} copy(bf16[4,8,4096]{2,1,0:T(8,128)(2,1)} %harvest.1) | data formatting | bytes 524288

commit v2 on v1

--- a/solution.py
+++ b/solution.py
@@ -12,8 +12,8 @@
 SUBLANES = 8
 
 
-def harvest_kernel(sections, groups, x_hbm, owners, out_ref, inverse, xv, centered, part, parts, s1, s2, r2,
-                   x_sem, e_send, e_recv, send1, recv1, send2, recv2, *r1):
+def harvest_kernel(sections, groups, early, x_hbm, owners_hbm, out_ref, owners, inverse, xv, centered, part, parts,
+                   s1, s2, r2, x_sem, o_sem, e_send, e_recv, send1, recv1, send2, recv2, *r1):
     layers, tokens, features = x_hbm.shape
     chunks, blocks, rows, _ = s1.shape
     width = features // groups
@@ -35,15 +35,18 @@
     for k in range(1, sections):
         pl.semaphore_signal(barrier, inc=1, device_id=(lax.rem(section + k, sections), group), device_id_type=MESH)
 
+    load_owners = pltpu.make_async_copy(owners_hbm, owners, o_sem)
+    load_owners.start()
     load.wait()
     per_tile = SUBLANES // layers
     acc = jnp.zeros((SUBLANES, LANES), jnp.float32)
     for g in range(tokens // per_tile):
         x8 = jnp.concatenate([xv[:, g * per_tile + i, :] for i in range(per_tile)], axis=0)
         c = x8 - jnp.sum(x8, axis=1, keepdims=True) * (1.0 / features)
-        centered[g * SUBLANES:(g + 1) * SUBLANES, :] = c
+        j, r = divmod(g * SUBLANES, rows)
         sq = c * c
         for f in range(features // LANES):
+            centered[f, j, r:r + SUBLANES] = c[:, f * LANES:(f + 1) * LANES]
             acc = acc + sq[:, f * LANES:(f + 1) * LANES]
     part[...] = acc
     parts[group] = acc
@@ -53,6 +56,21 @@
         pltpu.make_async_remote_copy(
             src_ref=part, dst_ref=parts.at[group], send_sem=e_send, recv_sem=e_recv,
             device_id=(section, peer_of(k)), device_id_type=MESH).start()
+
+    mine = pl.ds(group * per_dev, per_dev)
+
+    def spread(k, source):
+        for p in range(1, groups):
+            d = peer_of(p)
+            pltpu.make_async_remote_copy(
+                src_ref=source(d), dst_ref=r1[k].at[mine], send_sem=send1.at[k], recv_sem=recv1.at[k],
+                device_id=(section, d), device_id_type=MESH).start()
+        r1[k][mine] = source(group)[...]
+
+    for k in range(early):
+        spread(k, lambda d: centered.at[d * chunks + k])
+
+    load_owners.wait()
 
     @pl.loop(0, blocks)
     def _(o):
@@ -76,20 +94,11 @@
     scale = 1.0 / jnp.sqrt(energy * (1.0 / (tokens * groups * features)) + 1.0)
     scale = jnp.concatenate([scale] * (rows // SUBLANES), axis=0)
 
-    for k in range(chunks):
+    for k in range(early, chunks):
         for d in range(groups):
             for j in range(per_dev):
-                lane = d * width + k * LANES
-                s1[k, d * per_dev + j] = (
-                    centered[j * rows:(j + 1) * rows, lane:lane + LANES] * scale).astype(jnp.bfloat16)
-        mine = pl.ds(group * per_dev, per_dev)
-        for p in range(1, groups):
-            d = peer_of(p)
-            pltpu.make_async_remote_copy(
-                src_ref=s1.at[k, pl.ds(d * per_dev, per_dev)], dst_ref=r1[k].at[mine],
-                send_sem=send1.at[k], recv_sem=recv1.at[k],
-                device_id=(section, d), device_id_type=MESH).start()
-        r1[k][mine] = s1[k, mine]
+                s1[k, d * per_dev + j] = (centered[d * chunks + k, j] * scale).astype(jnp.bfloat16)
+        spread(k, lambda d: s1.at[k, pl.ds(d * per_dev, per_dev)])
 
     for k in range(chunks):
         span = pl.ds(0, (groups - 1) * per_dev)
@@ -97,7 +106,8 @@
             src_ref=r1[k].at[span], dst_ref=r1[k].at[span], send_sem=send1.at[k], recv_sem=recv1.at[k],
             device_id=(section, peer_of(1)), device_id_type=MESH).wait_recv()
         for o in range(devices):
-            s2[k, o] = r1[k][inverse[o]]
+            block = r1[k][inverse[o]]
+            s2[k, o] = (block * scale).astype(jnp.bfloat16) if k < early else block
         for p in range(1, devices):
             o = lax.rem(me + p, devices)
             pltpu.make_async_remote_copy(
@@ -122,7 +132,7 @@
     for k in range(chunks):
         span = pl.ds(0, (groups - 1) * per_dev)
         pltpu.make_async_remote_copy(
-            src_ref=s1.at[k, span], dst_ref=r1[k].at[span], send_sem=send1.at[k], recv_sem=recv1.at[k],
+            src_ref=r1[k].at[span], dst_ref=r1[k].at[span], send_sem=send1.at[k], recv_sem=recv1.at[k],
             device_id=(section, peer_of(1)), device_id_type=MESH).wait_send()
         span = pl.ds(0, devices - 1)
         pltpu.make_async_remote_copy(
@@ -139,25 +149,27 @@
         block_len = tokens * groups // blocks
         rows = block_len * layers
         chunks = features // groups // LANES
+        early = chunks // 2
         tiles = (chunks, blocks, rows, LANES)
         dma = pltpu.SemaphoreType.DMA
         return pl.pallas_call(
-            functools.partial(harvest_kernel, sections, groups),
+            functools.partial(harvest_kernel, sections, groups, early),
             out_shape=jax.ShapeDtypeStruct((block_len, layers * sections, features), jnp.bfloat16),
-            in_specs=[pl.BlockSpec(memory_space=pl.ANY), pl.BlockSpec(memory_space=pltpu.SMEM)],
+            in_specs=[pl.BlockSpec(memory_space=pl.ANY), pl.BlockSpec(memory_space=pl.ANY)],
             out_specs=pl.BlockSpec(memory_space=pltpu.VMEM),
             scratch_shapes=[
                 pltpu.SMEM((blocks,), jnp.int32),
+                pltpu.SMEM((blocks,), jnp.int32),
                 pltpu.VMEM((layers, tokens, features), jnp.float32),
-                pltpu.VMEM((layers * tokens, features), jnp.float32),
+                pltpu.VMEM((features // LANES, blocks // groups, rows, LANES), jnp.float32),
                 pltpu.VMEM((SUBLANES, LANES), jnp.float32),
                 pltpu.VMEM((groups, SUBLANES, LANES), jnp.float32),
                 pltpu.VMEM(tiles, jnp.bfloat16),
                 pltpu.VMEM(tiles, jnp.bfloat16),
                 pltpu.VMEM(tiles, jnp.bfloat16),
-                dma, dma, dma,
+                dma, dma, dma, dma,
                 dma((chunks,)), dma((chunks,)), dma((chunks,)), dma((chunks,)),
-                *[pltpu.VMEM(tiles[1:], jnp.bfloat16) for _ in range(chunks)],
+                *[pltpu.VMEM(tiles[1:], jnp.float32 if k < early else jnp.bfloat16) for k in range(chunks)],
             ],
             compiler_params=pltpu.CompilerParams(collective_id=0, has_side_effects=True),
             name="harvest",

time: 27.1 us -> 27.8 us (1.026)
  Pallas kernels: 25.3 us -> 26 us
    pallas_call x1, Pallas kernels: 25.3 us -> 26 us  [on_device(): pl.pallas_call(functools.partial(harvest_kernel, sections, groups, early)...]
where the time goes in v2:
time: 27.8 us; the launch traced here: 27.7 us
  Pallas kernels  26 us (94%)
  local copies, waits for them, and re-layouts  1.67 us (6%)
    pallas_call x1, Pallas kernels, on_device(): pl.pallas_call(functools.partial(harvest_kernel, sections, groups, early)...  26 us
    unnamed x1, local copies, waits for them, and re-layouts  1.67 us

profile of v2, /device:TPU:0, one launch (start us, length us, event | category | flops | bytes accessed | tf_op | source)
XLA Modules:
  0.0 27.7 jit_solution(6703167410824587347)
XLA Ops:
  0.0 26.0 %harvest.1 = bf16[4,8,4096]{2,1,0:T(8,128)(2,1)} custom-call(f32[4,8,4096]{2,1,0:T(8,128)} %x_hbm.1, s32[32]{0:T(128)} %owners_hbm.1), custom_call_target="tpu_custom_call" | custom-call | tf_op jit(solution)/shard_map/harvest/pallas_call | solution.py:155
  26.0 1.7 %copy.4 = bf16[4,8,4096]{2,1,0:T(8,128)(2,1)} copy(bf16[4,8,4096]{2,1,0:T(8,128)(2,1)} %harvest.1) | data formatting | bytes 524288

commit v3 on v2

--- a/solution.py
+++ b/solution.py
@@ -12,8 +12,8 @@
 SUBLANES = 8
 
 
-def harvest_kernel(sections, groups, early, x_hbm, owners_hbm, out_ref, owners, inverse, xv, centered, part, parts,
-                   s1, s2, r2, x_sem, o_sem, e_send, e_recv, send1, recv1, send2, recv2, *r1):
+def harvest_kernel(sections, groups, early, x_hbm, owners_hbm, r2, owners, inverse, xv, centered, part, parts,
+                   s1, s2, x_sem, o_sem, e_send, e_recv, send1, recv1, send2, recv2, *r1):
     layers, tokens, features = x_hbm.shape
     chunks, blocks, rows, _ = s1.shape
     width = features // groups
@@ -121,13 +121,6 @@
         pltpu.make_async_remote_copy(
             src_ref=r2.at[k, span], dst_ref=r2.at[k, span], send_sem=send2.at[k], recv_sem=recv2.at[k],
             device_id=(section, peer_of(1)), device_id_type=MESH).wait_recv()
-        for d in range(groups):
-            got = [r2[k, s * groups + d].astype(jnp.float32) for s in range(sections)]
-            lane = d * width + k * LANES
-            for i in range(block_len):
-                out_ref[i, :, lane:lane + LANES] = jnp.concatenate(
-                    [v[i * layers:(i + 1) * layers] for v in got], axis=0).astype(jnp.bfloat16)
-
     energy_wait.wait_send()
     for k in range(chunks):
         span = pl.ds(0, (groups - 1) * per_dev)
@@ -140,6 +133,20 @@
             device_id=(section, peer_of(1)), device_id_type=MESH).wait_send()
 
 
+def assemble_kernel(sections, groups, r2, out_ref):
+    block_len, all_layers, features = out_ref.shape
+    layers = all_layers // sections
+    chunks = r2.shape[0]
+    width = features // groups
+    for k in range(chunks):
+        for d in range(groups):
+            got = [r2[k, s * groups + d].astype(jnp.float32) for s in range(sections)]
+            lane = d * width + k * LANES
+            for i in range(block_len):
+                out_ref[i, :, lane:lane + LANES] = jnp.concatenate(
+                    [v[i * layers:(i + 1) * layers] for v in got], axis=0).astype(jnp.bfloat16)
+
+
 def solution(mesh):
     sections, groups = mesh.shape["section"], mesh.shape["dp"]
 
@@ -149,12 +156,12 @@
         block_len = tokens * groups // blocks
         rows = block_len * layers
         chunks = features // groups // LANES
-        early = chunks // 2
+        early = 0
         tiles = (chunks, blocks, rows, LANES)
         dma = pltpu.SemaphoreType.DMA
-        return pl.pallas_call(
+        received = pl.pallas_call(
             functools.partial(harvest_kernel, sections, groups, early),
-            out_shape=jax.ShapeDtypeStruct((block_len, layers * sections, features), jnp.bfloat16),
+            out_shape=pltpu.VMEM(tiles, jnp.bfloat16),
             in_specs=[pl.BlockSpec(memory_space=pl.ANY), pl.BlockSpec(memory_space=pl.ANY)],
             out_specs=pl.BlockSpec(memory_space=pltpu.VMEM),
             scratch_shapes=[
@@ -166,7 +173,6 @@
                 pltpu.VMEM((groups, SUBLANES, LANES), jnp.float32),
                 pltpu.VMEM(tiles, jnp.bfloat16),
                 pltpu.VMEM(tiles, jnp.bfloat16),
-                pltpu.VMEM(tiles, jnp.bfloat16),
                 dma, dma, dma, dma,
                 dma((chunks,)), dma((chunks,)), dma((chunks,)), dma((chunks,)),
                 *[pltpu.VMEM(tiles[1:], jnp.float32 if k < early else jnp.bfloat16) for k in range(chunks)],
@@ -174,6 +180,13 @@
             compiler_params=pltpu.CompilerParams(collective_id=0, has_side_effects=True),
             name="harvest",
         )(residuals, owners)
+        return pl.pallas_call(
+            functools.partial(assemble_kernel, sections, groups),
+            out_shape=jax.ShapeDtypeStruct((block_len, layers * sections, features), jnp.bfloat16),
+            in_specs=[pl.BlockSpec(memory_space=pltpu.VMEM)],
+            out_specs=pl.BlockSpec(memory_space=pltpu.VMEM),
+            name="assemble",
+        )(pltpu.with_memory_space_constraint(received, pltpu.VMEM))
 
     in_specs = (P("section", "dp", None), P())
     out_specs = P(("section", "dp"), None, None)

time: 27.8 us -> 24.8 us (0.89)
  local copies, waits for them, and re-layouts: 1.67 us -> 0 us
  Pallas kernels: 26 us -> 24.6 us
    pallas_call x1, Pallas kernels: 26 us -> 23.9 us  [on_device(): pl.pallas_call(functools.partial(harvest_kernel, sections, groups, early)...]
    unnamed x1 -> x0, local copies, waits for them, and re-layouts: 1.67 us -> none
    pallas_call x0 -> x1, Pallas kernels: none -> 0.77 us  [on_device(): pl.pallas_call(functools.partial(assemble_kernel, sections, groups), out_...]
where the time goes in v3:
time: 24.8 us; the launch traced here: 24.6 us
  Pallas kernels  24.6 us (99%)
    pallas_call x1, Pallas kernels, on_device(): pl.pallas_call(functools.partial(harvest_kernel, sections, groups, early)...  23.9 us
    pallas_call x1, Pallas kernels, on_device(): pl.pallas_call(functools.partial(assemble_kernel, sections, groups), out_...  0.77 us

profile of v3, /device:TPU:0, one launch (start us, length us, event | category | flops | bytes accessed | tf_op | source)
XLA Modules:
  0.0 24.6 jit_solution(1238993238983993219)
XLA Ops:
  0.0 23.9 %harvest.1.r2 = bf16[2,32,16,128]{3,2,1,0:T(8,128)(2,1)S(1)} custom-call(f32[4,8,4096]{2,1,0:T(8,128)} %x_hbm.1, s32[32]{0:T(128)} %owners_hbm.1), custom_call_target="tpu_custom_call" | custom-call | tf_op jit(solution)/shard_map/harvest/pallas_call | solution.py:162
  23.9 0.8 %assemble.1 = bf16[4,8,4096]{2,1,0:T(8,128)(2,1)} custom-call(bf16[2,32,16,128]{3,2,1,0:T(8,128)(2,1)S(1)} %harvest.1.r2), custom_call_target="tpu_custom_call" | custom-call | tf_op jit(solution)/shard_map/assemble/pallas_call | solution.py:183

commit v4 on v3

--- a/solution.py
+++ b/solution.py
@@ -48,11 +48,20 @@
         for f in range(features // LANES):
             centered[f, j, r:r + SUBLANES] = c[:, f * LANES:(f + 1) * LANES]
             acc = acc + sq[:, f * LANES:(f + 1) * LANES]
+    lane = lax.broadcasted_iota(jnp.int32, (SUBLANES, LANES), 1)
+    row = lax.broadcasted_iota(jnp.int32, (SUBLANES, LANES), 0)
+    own_lanes = lane // (LANES // layers) == row % layers
+    fold = LANES // 2
+    while fold >= LANES // layers:
+        acc = acc + pltpu.roll(acc, fold, 1)
+        fold //= 2
+    acc = jnp.sum(jnp.where(own_lanes, acc, 0.0), axis=0, keepdims=True)
     part[...] = acc
     parts[group] = acc
 
     pl.semaphore_wait(barrier, groups + sections - 2)
-    for k in range(1, groups):
+    order = sorted(range(1, groups), key=lambda p: min(p, groups - p))
+    for k in order:
         pltpu.make_async_remote_copy(
             src_ref=part, dst_ref=parts.at[group], send_sem=e_send, recv_sem=e_recv,
             device_id=(section, peer_of(k)), device_id_type=MESH).start()
@@ -60,7 +69,7 @@
     mine = pl.ds(group * per_dev, per_dev)
 
     def spread(k, source):
-        for p in range(1, groups):
+        for p in order:
             d = peer_of(p)
             pltpu.make_async_remote_copy(
                 src_ref=source(d), dst_ref=r1[k].at[mine], send_sem=send1.at[k], recv_sem=recv1.at[k],
@@ -87,10 +96,7 @@
     total = parts[0]
     for g in range(1, groups):
         total = total + parts[g]
-    row = jnp.sum(total, axis=1, keepdims=True)
-    energy = row
-    for i in range(1, per_tile):
-        energy = energy + jnp.concatenate([row[i * layers:], row[:i * layers]], axis=0)
+    energy = jnp.sum(jnp.where(own_lanes, total, 0.0), axis=1, keepdims=True)
     scale = 1.0 / jnp.sqrt(energy * (1.0 / (tokens * groups * features)) + 1.0)
     scale = jnp.concatenate([scale] * (rows // SUBLANES), axis=0)
 
@@ -108,12 +114,13 @@
         for o in range(devices):
             block = r1[k][inverse[o]]
             s2[k, o] = (block * scale).astype(jnp.bfloat16) if k < early else block
-        for p in range(1, devices):
-            o = lax.rem(me + p, devices)
+        for p, q in [(p, q) for p in order + [0] for q in range(sections) if p or q]:
+            sec, d = lax.rem(section + q, sections), peer_of(p)
+            o = sec * groups + d
             pltpu.make_async_remote_copy(
                 src_ref=s2.at[k, o], dst_ref=r2.at[k, me],
                 send_sem=send2.at[k], recv_sem=recv2.at[k],
-                device_id=(o // groups, lax.rem(o, groups)), device_id_type=MESH).start()
+                device_id=(sec, d), device_id_type=MESH).start()
         r2[k, me] = s2[k, me]
 
     for k in range(chunks):
@@ -169,8 +176,8 @@
                 pltpu.SMEM((blocks,), jnp.int32),
                 pltpu.VMEM((layers, tokens, features), jnp.float32),
                 pltpu.VMEM((features // LANES, blocks // groups, rows, LANES), jnp.float32),
-                pltpu.VMEM((SUBLANES, LANES), jnp.float32),
-                pltpu.VMEM((groups, SUBLANES, LANES), jnp.float32),
+                pltpu.VMEM((1, LANES), jnp.float32),
+                pltpu.VMEM((groups, 1, LANES), jnp.float32),
                 pltpu.VMEM(tiles, jnp.bfloat16),
                 pltpu.VMEM(tiles, jnp.bfloat16),
                 dma, dma, dma, dma,

time: 24.8 us -> 24.1 us (0.972)
  Pallas kernels: 24.6 us -> 24 us
    pallas_call x1, Pallas kernels: 23.9 us -> 23.2 us  [on_device(): pl.pallas_call(functools.partial(harvest_kernel, sections, groups, early)...]
where the time goes in v4:
time: 24.1 us; the launch traced here: 24 us
  Pallas kernels  24 us (100%)
    pallas_call x1, Pallas kernels, on_device(): pl.pallas_call(functools.partial(harvest_kernel, sections, groups, early)...  23.2 us
    pallas_call x1, Pallas kernels, on_device(): pl.pallas_call(functools.partial(assemble_kernel, sections, groups), out_...  0.77 us

profile of v4, /device:TPU:0, one launch (start us, length us, event | category | flops | bytes accessed | tf_op | source)
XLA Modules:
  0.0 24.0 jit_solution(14967182541395906812)
XLA Ops:
  0.0 23.2 %harvest.1.r2 = bf16[2,32,16,128]{3,2,1,0:T(8,128)(2,1)S(1)} custom-call(f32[4,8,4096]{2,1,0:T(8,128)} %x_hbm.1, s32[32]{0:T(128)} %owners_hbm.1), custom_call_target="tpu_custom_call" | custom-call | tf_op jit(solution)/shard_map/harvest/pallas_call | solution.py:169
  23.2 0.8 %assemble.1 = bf16[4,8,4096]{2,1,0:T(8,128)(2,1)} custom-call(bf16[2,32,16,128]{3,2,1,0:T(8,128)(2,1)S(1)} %harvest.1.r2), custom_call_target="tpu_custom_call" | custom-call | tf_op jit(solution)/shard_map/assemble/pallas_call | solution.py:190

commit v5 on v4

--- a/solution.py
+++ b/solution.py
@@ -12,8 +12,9 @@
 SUBLANES = 8
 
 
-def harvest_kernel(sections, groups, early, x_hbm, owners_hbm, r2, owners, inverse, xv, centered, part, parts,
-                   s1, s2, x_sem, o_sem, e_send, e_recv, send1, recv1, send2, recv2, *r1):
+def harvest_kernel(sections, groups, early, x_hbm, owners_hbm, out_ref, owners, inverse, xv, centered, part, parts,
+                   late, s1, s2, r2, x_sem, o_sem, e_send, e_recv, send1, recv1, send2, recv2, *r1):
+    half = s1.shape[2] // 2
     layers, tokens, features = x_hbm.shape
     chunks, blocks, rows, _ = s1.shape
     width = features // groups
@@ -61,23 +62,27 @@
 
     pl.semaphore_wait(barrier, groups + sections - 2)
     order = sorted(range(1, groups), key=lambda p: min(p, groups - p))
+    early_order = sorted(range(1, groups), key=lambda p: min(p, groups - p))
+    first_order = sorted(range(1, groups), key=lambda p: min(p, groups - p))
+    second_order = list(range(1, groups))
     for k in order:
         pltpu.make_async_remote_copy(
             src_ref=part, dst_ref=parts.at[group], send_sem=e_send, recv_sem=e_recv,
             device_id=(section, peer_of(k)), device_id_type=MESH).start()
 
     mine = pl.ds(group * per_dev, per_dev)
-
-    def spread(k, source):
-        for p in order:
+    units = len(r1)
+
+    def spread(u, source):
+        for p in (early_order if u == chunks else first_order):
             d = peer_of(p)
             pltpu.make_async_remote_copy(
-                src_ref=source(d), dst_ref=r1[k].at[mine], send_sem=send1.at[k], recv_sem=recv1.at[k],
+                src_ref=source(d), dst_ref=r1[u].at[mine], send_sem=send1.at[u], recv_sem=recv1.at[u],
                 device_id=(section, d), device_id_type=MESH).start()
-        r1[k][mine] = source(group)[...]
-
-    for k in range(early):
-        spread(k, lambda d: centered.at[d * chunks + k])
+        r1[u][mine] = source(group)[...]
+
+    if early:
+        spread(chunks, lambda d: centered.at[d * chunks, :, pl.ds(0, half)])
 
     load_owners.wait()
 
@@ -100,21 +105,38 @@
     scale = 1.0 / jnp.sqrt(energy * (1.0 / (tokens * groups * features)) + 1.0)
     scale = jnp.concatenate([scale] * (rows // SUBLANES), axis=0)
 
-    for k in range(early, chunks):
+    for k in range(chunks):
+        top = half if early and k == 0 else 0
         for d in range(groups):
             for j in range(per_dev):
-                s1[k, d * per_dev + j] = (centered[d * chunks + k, j] * scale).astype(jnp.bfloat16)
-        spread(k, lambda d: s1.at[k, pl.ds(d * per_dev, per_dev)])
-
-    for k in range(chunks):
+                b = d * per_dev + j
+                if top:
+                    late[b] = (centered[d * chunks, j, top:] * scale[top:]).astype(jnp.bfloat16)
+                else:
+                    s1[k, b] = (centered[d * chunks + k, j] * scale).astype(jnp.bfloat16)
+        if top:
+            spread(k, lambda d: late.at[pl.ds(d * per_dev, per_dev)])
+        else:
+            spread(k, lambda d: s1.at[k, pl.ds(d * per_dev, per_dev)])
+
+    def arrived(u):
         span = pl.ds(0, (groups - 1) * per_dev)
-        pltpu.make_async_remote_copy(
-            src_ref=r1[k].at[span], dst_ref=r1[k].at[span], send_sem=send1.at[k], recv_sem=recv1.at[k],
-            device_id=(section, peer_of(1)), device_id_type=MESH).wait_recv()
+        return pltpu.make_async_remote_copy(
+            src_ref=r1[u].at[span], dst_ref=r1[u].at[span], send_sem=send1.at[u], recv_sem=recv1.at[u],
+            device_id=(section, peer_of(1)), device_id_type=MESH)
+
+    if early:
+        arrived(chunks).wait_recv()
+    for k in range(chunks):
+        arrived(k).wait_recv()
         for o in range(devices):
-            block = r1[k][inverse[o]]
-            s2[k, o] = (block * scale).astype(jnp.bfloat16) if k < early else block
-        for p, q in [(p, q) for p in order + [0] for q in range(sections) if p or q]:
+            b = inverse[o]
+            if early and k == 0:
+                first = r1[chunks][b] * scale[:half]
+                s2[k, o] = jnp.concatenate([first, r1[k][b].astype(jnp.float32)], axis=0).astype(jnp.bfloat16)
+            else:
+                s2[k, o] = r1[k][b]
+        for p, q in [(p, q) for p in second_order + [0] for q in range(sections) if p or q]:
             sec, d = lax.rem(section + q, sections), peer_of(p)
             o = sec * groups + d
             pltpu.make_async_remote_copy(
@@ -128,30 +150,26 @@
         pltpu.make_async_remote_copy(
             src_ref=r2.at[k, span], dst_ref=r2.at[k, span], send_sem=send2.at[k], recv_sem=recv2.at[k],
             device_id=(section, peer_of(1)), device_id_type=MESH).wait_recv()
-    energy_wait.wait_send()
-    for k in range(chunks):
-        span = pl.ds(0, (groups - 1) * per_dev)
-        pltpu.make_async_remote_copy(
-            src_ref=r1[k].at[span], dst_ref=r1[k].at[span], send_sem=send1.at[k], recv_sem=recv1.at[k],
-            device_id=(section, peer_of(1)), device_id_type=MESH).wait_send()
-        span = pl.ds(0, devices - 1)
-        pltpu.make_async_remote_copy(
-            src_ref=s2.at[k, span], dst_ref=r2.at[k, span], send_sem=send2.at[k], recv_sem=recv2.at[k],
-            device_id=(section, peer_of(1)), device_id_type=MESH).wait_send()
-
-
-def assemble_kernel(sections, groups, r2, out_ref):
-    block_len, all_layers, features = out_ref.shape
-    layers = all_layers // sections
-    chunks = r2.shape[0]
-    width = features // groups
-    for k in range(chunks):
         for d in range(groups):
             got = [r2[k, s * groups + d].astype(jnp.float32) for s in range(sections)]
             lane = d * width + k * LANES
             for i in range(block_len):
                 out_ref[i, :, lane:lane + LANES] = jnp.concatenate(
                     [v[i * layers:(i + 1) * layers] for v in got], axis=0).astype(jnp.bfloat16)
+    energy_wait.wait_send()
+    for u in range(units):
+        arrived(u).wait_send()
+    for k in range(chunks):
+        span = pl.ds(0, devices - 1)
+        pltpu.make_async_remote_copy(
+            src_ref=s2.at[k, span], dst_ref=r2.at[k, span], send_sem=send2.at[k], recv_sem=recv2.at[k],
+            device_id=(section, peer_of(1)), device_id_type=MESH).wait_send()
+
+
+def store_kernel(assembled, out_hbm, sem):
+    store = pltpu.make_async_copy(assembled, out_hbm, sem)
+    store.start()
+    store.wait()
 
 
 def solution(mesh):
@@ -163,12 +181,13 @@
         block_len = tokens * groups // blocks
         rows = block_len * layers
         chunks = features // groups // LANES
-        early = 0
+        early = chunks > 1
         tiles = (chunks, blocks, rows, LANES)
+        part_tiles = (blocks, rows // 2, LANES)
         dma = pltpu.SemaphoreType.DMA
         received = pl.pallas_call(
             functools.partial(harvest_kernel, sections, groups, early),
-            out_shape=pltpu.VMEM(tiles, jnp.bfloat16),
+            out_shape=pltpu.VMEM((block_len, layers * sections, features), jnp.bfloat16),
             in_specs=[pl.BlockSpec(memory_space=pl.ANY), pl.BlockSpec(memory_space=pl.ANY)],
             out_specs=pl.BlockSpec(memory_space=pltpu.VMEM),
             scratch_shapes=[
@@ -178,21 +197,26 @@
                 pltpu.VMEM((features // LANES, blocks // groups, rows, LANES), jnp.float32),
                 pltpu.VMEM((1, LANES), jnp.float32),
                 pltpu.VMEM((groups, 1, LANES), jnp.float32),
+                pltpu.VMEM(part_tiles, jnp.bfloat16),
+                pltpu.VMEM(tiles, jnp.bfloat16),
                 pltpu.VMEM(tiles, jnp.bfloat16),
                 pltpu.VMEM(tiles, jnp.bfloat16),
                 dma, dma, dma, dma,
-                dma((chunks,)), dma((chunks,)), dma((chunks,)), dma((chunks,)),
-                *[pltpu.VMEM(tiles[1:], jnp.float32 if k < early else jnp.bfloat16) for k in range(chunks)],
+                dma((chunks + early,)), dma((chunks + early,)), dma((chunks,)), dma((chunks,)),
+                *([pltpu.VMEM(part_tiles, jnp.bfloat16)] if early else []),
+                *[pltpu.VMEM(tiles[1:], jnp.bfloat16)] * (chunks - early),
+                *([pltpu.VMEM(part_tiles, jnp.float32)] if early else []),
             ],
             compiler_params=pltpu.CompilerParams(collective_id=0, has_side_effects=True),
             name="harvest",
         )(residuals, owners)
         return pl.pallas_call(
-            functools.partial(assemble_kernel, sections, groups),
-            out_shape=jax.ShapeDtypeStruct((block_len, layers * sections, features), jnp.bfloat16),
+            store_kernel,
+            out_shape=jax.ShapeDtypeStruct(received.shape, received.dtype),
             in_specs=[pl.BlockSpec(memory_space=pltpu.VMEM)],
-            out_specs=pl.BlockSpec(memory_space=pltpu.VMEM),
-            name="assemble",
+            out_specs=pl.BlockSpec(memory_space=pl.ANY),
+            scratch_shapes=[pltpu.SemaphoreType.DMA],
+            name="store",
         )(pltpu.with_memory_space_constraint(received, pltpu.VMEM))
 
     in_specs = (P("section", "dp", None), P())

time: 24.1 us -> 23.4 us (0.971)
  Pallas kernels: 24 us -> 23.3 us
    pallas_call x1, Pallas kernels: 23.2 us -> 22.6 us  [on_device(): pl.pallas_call(functools.partial(harvest_kernel, sections, groups, early)...]
where the time goes in v5:
time: 23.4 us; the launch traced here: 23.3 us
  Pallas kernels  23.3 us (100%)
    pallas_call x1, Pallas kernels, on_device(): pl.pallas_call(functools.partial(harvest_kernel, sections, groups, early)...  22.6 us
    pallas_call x1, Pallas kernels, on_device(): pl.pallas_call(store_kernel, out_shape=jax.ShapeDtypeStruct(received.shap...  0.71 us

profile of v5, /device:TPU:0, one launch (start us, length us, event | category | flops | bytes accessed | tf_op | source)
XLA Modules:
  0.0 23.3 jit_solution(8843778629123638357)
XLA Ops:
  0.0 22.6 %harvest.1.assembled = bf16[4,8,4096]{2,1,0:T(8,128)(2,1)S(1)} custom-call(f32[4,8,4096]{2,1,0:T(8,128)} %x_hbm.1, s32[32]{0:T(128)} %owners_hbm.1), custom_call_target="tpu_custom_call" | custom-call | tf_op jit(solution)/shard_map/harvest/pallas_call | solution.py:188
  22.6 0.7 %store.1 = bf16[4,8,4096]{2,1,0:T(8,128)(2,1)} custom-call(bf16[4,8,4096]{2,1,0:T(8,128)(2,1)S(1)} %harvest.1.assembled), custom_call_target="tpu_custom_call" | custom-call | tf_op jit(solution)/shard_map/store/pallas_call | solution.py:213

commit v6 on v5

--- a/solution.py
+++ b/solution.py
@@ -40,23 +40,25 @@
     load_owners.start()
     load.wait()
     per_tile = SUBLANES // layers
-    acc = jnp.zeros((SUBLANES, LANES), jnp.float32)
-    for g in range(tokens // per_tile):
-        x8 = jnp.concatenate([xv[:, g * per_tile + i, :] for i in range(per_tile)], axis=0)
-        c = x8 - jnp.sum(x8, axis=1, keepdims=True) * (1.0 / features)
-        j, r = divmod(g * SUBLANES, rows)
-        sq = c * c
-        for f in range(features // LANES):
-            centered[f, j, r:r + SUBLANES] = c[:, f * LANES:(f + 1) * LANES]
-            acc = acc + sq[:, f * LANES:(f + 1) * LANES]
     lane = lax.broadcasted_iota(jnp.int32, (SUBLANES, LANES), 1)
     row = lax.broadcasted_iota(jnp.int32, (SUBLANES, LANES), 0)
+    total = jnp.zeros((SUBLANES, LANES), jnp.float32)
+    for l in range(layers):
+        acc = jnp.zeros((SUBLANES, LANES), jnp.float32)
+        for t in range(0, tokens, SUBLANES):
+            x = xv[l, t:t + SUBLANES]
+            c = x - jnp.sum(x, axis=1, keepdims=True) * (1.0 / features)
+            xv[l, t:t + SUBLANES] = c
+            sq = c * c
+            for f in range(features // LANES):
+                acc = acc + sq[:, f * LANES:(f + 1) * LANES]
+        fold = LANES // 2
+        while fold >= LANES // layers:
+            acc = acc + pltpu.roll(acc, fold, 1)
+            fold //= 2
+        total = total + jnp.where(lane // (LANES // layers) == l, acc, 0.0)
     own_lanes = lane // (LANES // layers) == row % layers
-    fold = LANES // 2
-    while fold >= LANES // layers:
-        acc = acc + pltpu.roll(acc, fold, 1)
-        fold //= 2
-    acc = jnp.sum(jnp.where(own_lanes, acc, 0.0), axis=0, keepdims=True)
+    acc = jnp.sum(total, axis=0, keepdims=True)
     part[...] = acc
     parts[group] = acc
 
@@ -81,9 +83,22 @@
                 device_id=(section, d), device_id_type=MESH).start()
         r1[u][mine] = source(group)[...]
 
+    def regroup(g):
+        j, r = divmod(g * SUBLANES, rows)
+        c = jnp.concatenate([xv[:, g * per_tile + i, :] for i in range(per_tile)], axis=0)
+        for f in range(features // LANES):
+            centered[f, j, r:r + SUBLANES] = c[:, f * LANES:(f + 1) * LANES]
+
+    tiles = range(tokens // per_tile)
+    first = [g for g in tiles if g * SUBLANES % rows < half]
+    for g in first:
+        regroup(g)
     if early:
         spread(chunks, lambda d: centered.at[d * chunks, :, pl.ds(0, half)])
 
+    for g in tiles:
+        if g not in first:
+            regroup(g)
     load_owners.wait()
 
     @pl.loop(0, blocks)
@@ -125,31 +140,40 @@
             src_ref=r1[u].at[span], dst_ref=r1[u].at[span], send_sem=send1.at[u], recv_sem=recv1.at[u],
             device_id=(section, peer_of(1)), device_id_type=MESH)
 
-    if early:
-        arrived(chunks).wait_recv()
-    for k in range(chunks):
-        arrived(k).wait_recv()
-        for o in range(devices):
-            b = inverse[o]
-            if early and k == 0:
-                first = r1[chunks][b] * scale[:half]
-                s2[k, o] = jnp.concatenate([first, r1[k][b].astype(jnp.float32)], axis=0).astype(jnp.bfloat16)
-            else:
-                s2[k, o] = r1[k][b]
+    def deliver(u, view):
         for p, q in [(p, q) for p in second_order + [0] for q in range(sections) if p or q]:
             sec, d = lax.rem(section + q, sections), peer_of(p)
-            o = sec * groups + d
             pltpu.make_async_remote_copy(
-                src_ref=s2.at[k, o], dst_ref=r2.at[k, me],
-                send_sem=send2.at[k], recv_sem=recv2.at[k],
+                src_ref=view(s2, sec * groups + d), dst_ref=view(r2, me), send_sem=send2.at[u], recv_sem=recv2.at[u],
                 device_id=(sec, d), device_id_type=MESH).start()
-        r2[k, me] = s2[k, me]
+        view(r2, me)[...] = view(s2, me)[...]
+
+    def view_of(u):
+        if u == chunks:
+            return lambda ref, at: ref.at[0, at, pl.ds(0, half)]
+        if early and u == 0:
+            return lambda ref, at: ref.at[0, at, pl.ds(half, half)]
+        return lambda ref, at: ref.at[u, at]
+
+    def delivered(u):
+        ref = view_of(u)(r2, pl.ds(0, devices - 1))
+        return pltpu.make_async_remote_copy(
+            src_ref=ref, dst_ref=ref, send_sem=send2.at[u], recv_sem=recv2.at[u],
+            device_id=(section, peer_of(1)), device_id_type=MESH)
+
+    for u in ([chunks] if early else []) + list(range(chunks)):
+        arrived(u).wait_recv()
+        for o in range(devices):
+            block = r1[u][inverse[o]]
+            if u == chunks:
+                block = (block * scale[:half]).astype(jnp.bfloat16)
+            view_of(u)(s2, o)[...] = block
+        deliver(u, view_of(u))
 
     for k in range(chunks):
-        span = pl.ds(0, devices - 1)
-        pltpu.make_async_remote_copy(
-            src_ref=r2.at[k, span], dst_ref=r2.at[k, span], send_sem=send2.at[k], recv_sem=recv2.at[k],
-            device_id=(section, peer_of(1)), device_id_type=MESH).wait_recv()
+        delivered(k).wait_recv()
+        if early and k == 0:
+            delivered(chunks).wait_recv()
         for d in range(groups):
             got = [r2[k, s * groups + d].astype(jnp.float32) for s in range(sections)]
             lane = d * width + k * LANES
@@ -159,11 +183,7 @@
     energy_wait.wait_send()
     for u in range(units):
         arrived(u).wait_send()
-    for k in range(chunks):
-        span = pl.ds(0, devices - 1)
-        pltpu.make_async_remote_copy(
-            src_ref=s2.at[k, span], dst_ref=r2.at[k, span], send_sem=send2.at[k], recv_sem=recv2.at[k],
-            device_id=(section, peer_of(1)), device_id_type=MESH).wait_send()
+        delivered(u).wait_send()
 
 
 def store_kernel(assembled, out_hbm, sem):
@@ -202,7 +222,7 @@
                 pltpu.VMEM(tiles, jnp.bfloat16),
                 pltpu.VMEM(tiles, jnp.bfloat16),
                 dma, dma, dma, dma,
-                dma((chunks + early,)), dma((chunks + early,)), dma((chunks,)), dma((chunks,)),
+                *[dma((chunks + early,)) for _ in range(4)],
                 *([pltpu.VMEM(part_tiles, jnp.bfloat16)] if early else []),
                 *[pltpu.VMEM(tiles[1:], jnp.bfloat16)] * (chunks - early),
                 *([pltpu.VMEM(part_tiles, jnp.float32)] if early else []),

time: 23.4 us -> 23.1 us (0.987)
  Pallas kernels: 23.3 us -> 22.9 us
    pallas_call x1, Pallas kernels: 22.6 us -> 22.2 us  [on_device(): pl.pallas_call(functools.partial(harvest_kernel, sections, groups, early)...]
where the time goes in v6:
time: 23.1 us; the launch traced here: 22.9 us
  Pallas kernels  22.9 us (99%)
    pallas_call x1, Pallas kernels, on_device(): pl.pallas_call(functools.partial(harvest_kernel, sections, groups, early)...  22.2 us
    pallas_call x1, Pallas kernels, on_device(): pl.pallas_call(store_kernel, out_shape=jax.ShapeDtypeStruct(received.shap...  0.71 us

profile of v6, /device:TPU:0, one launch (start us, length us, event | category | flops | bytes accessed | tf_op | source)
XLA Modules:
  0.0 22.9 jit_solution(801116126993100265)
XLA Ops:
  0.0 22.2 %harvest.1.assembled = bf16[4,8,4096]{2,1,0:T(8,128)(2,1)S(1)} custom-call(f32[4,8,4096]{2,1,0:T(8,128)} %x_hbm.1, s32[32]{0:T(128)} %owners_hbm.1), custom_call_target="tpu_custom_call" | custom-call | tf_op jit(solution)/shard_map/harvest/pallas_call | solution.py:208
  22.2 0.7 %store.1 = bf16[4,8,4096]{2,1,0:T(8,128)(2,1)} custom-call(bf16[4,8,4096]{2,1,0:T(8,128)(2,1)S(1)} %harvest.1.assembled), custom_call_target="tpu_custom_call" | custom-call | tf_op jit(solution)/shard_map/store/pallas_call | solution.py:233

commit v7 on v6

--- a/solution.py
+++ b/solution.py
@@ -140,13 +140,33 @@
             src_ref=r1[u].at[span], dst_ref=r1[u].at[span], send_sem=send1.at[u], recv_sem=recv1.at[u],
             device_id=(section, peer_of(1)), device_id_type=MESH)
 
+    routes = [(p, q) for p in second_order + [0] for q in range(sections)]
+    lag = 8
+
     def deliver(u, view):
-        for p, q in [(p, q) for p in second_order + [0] for q in range(sections) if p or q]:
+        def place(p, q):
             sec, d = lax.rem(section + q, sections), peer_of(p)
-            pltpu.make_async_remote_copy(
-                src_ref=view(s2, sec * groups + d), dst_ref=view(r2, me), send_sem=send2.at[u], recv_sem=recv2.at[u],
-                device_id=(sec, d), device_id_type=MESH).start()
-        view(r2, me)[...] = view(s2, me)[...]
+            return sec, d, sec * groups + d
+
+        def select(p, q):
+            o = place(p, q)[2]
+            block = r1[u][inverse[o]]
+            if u == chunks:
+                block = (block * scale[:half]).astype(jnp.bfloat16)
+            view(s2 if p or q else r2, o)[...] = block
+
+        def send(p, q):
+            if p or q:
+                sec, d, o = place(p, q)
+                pltpu.make_async_remote_copy(
+                    src_ref=view(s2, o), dst_ref=view(r2, me), send_sem=send2.at[u], recv_sem=recv2.at[u],
+                    device_id=(sec, d), device_id_type=MESH).start()
+
+        for n in range(len(routes) + lag):
+            if n < len(routes):
+                select(*routes[n])
+            if n >= lag:
+                send(*routes[n - lag])
 
     def view_of(u):
         if u == chunks:
@@ -163,11 +183,6 @@
 
     for u in ([chunks] if early else []) + list(range(chunks)):
         arrived(u).wait_recv()
-        for o in range(devices):
-            block = r1[u][inverse[o]]
-            if u == chunks:
-                block = (block * scale[:half]).astype(jnp.bfloat16)
-            view_of(u)(s2, o)[...] = block
         deliver(u, view_of(u))
 
     for k in range(chunks):

time: 23.1 us -> 23.1 us (level)
  no operation moved by 1% of the time
where the time goes in v7:
time: 23.1 us; the launch traced here: 22.9 us
  Pallas kernels  22.9 us (99%)
    pallas_call x1, Pallas kernels, on_device(): pl.pallas_call(functools.partial(harvest_kernel, sections, groups, early)...  22.2 us
    pallas_call x1, Pallas kernels, on_device(): pl.pallas_call(store_kernel, out_shape=jax.ShapeDtypeStruct(received.shap...  0.71 us

profile of v7, /device:TPU:0, one launch (start us, length us, event | category | flops | bytes accessed | tf_op | source)
XLA Modules:
  0.0 22.9 jit_solution(2414268341785811284)
XLA Ops:
  0.0 22.2 %harvest.1.assembled = bf16[4,8,4096]{2,1,0:T(8,128)(2,1)S(1)} custom-call(f32[4,8,4096]{2,1,0:T(8,128)} %x_hbm.1, s32[32]{0:T(128)} %owners_hbm.1), custom_call_target="tpu_custom_call" | custom-call | tf_op jit(solution)/shard_map/harvest/pallas_call | solution.py:223
  22.2 0.7 %store.1 = bf16[4,8,4096]{2,1,0:T(8,128)(2,1)} custom-call(bf16[4,8,4096]{2,1,0:T(8,128)(2,1)S(1)} %harvest.1.assembled), custom_call_target="tpu_custom_call" | custom-call | tf_op jit(solution)/shard_map/store/pallas_call | solution.py:248
